TPU v7x, 32 devices: a whole 2x2x4 slice. The times are simulated.
32 devices in a mesh: dp: 4 (over z), ep: 8 (over y, x, core).
Axes of the slice: x: 2, y: 2, z: 4, core: 2. Of those that a mesh axis runs over, the one named last changes fastest.
Arguments:
- x_in: bfloat16 [32, 256, 1536], P(('dp', 'ep'))
- dy_in: bfloat16 [32, 256, 1536], P(('dp', 'ep'))
- route_idx: int32 [32, 256, 6], P(('dp', 'ep'))
- gain_attn: bfloat16 [1536], replicated
- w_qkv: bfloat16 [1536, 4608], replicated
- w_o: bfloat16 [1536, 1536], replicated
- gain_ffn: bfloat16 [1536], replicated
- w_router: bfloat16 [1536, 64], replicated
- w_up: bfloat16 [64, 1536, 512], P('ep')
- w_lin: bfloat16 [64, 1536, 512], P('ep')
- w_down: bfloat16 [64, 512, 1536], P('ep')
Outputs:
- output 1: bfloat16 [32, 256, 1536], P(('dp', 'ep'))
- output 2: float32 [1536], replicated
- output 3: float32 [1536, 4608], replicated
- output 4: float32 [1536, 1536], replicated
- output 5: float32 [1536], replicated
- output 6: float32 [1536, 64], replicated
- output 7: float32 [64, 1536, 512], P('ep')
- output 8: float32 [64, 1536, 512], P('ep')
- output 9: float32 [64, 512, 1536], P('ep')
All inputs are finite; a program needn't handle non-finite values.
Results may differ from a plain program's by a relative error of at most 0.017496.
Values are sent between devices in bfloat16 or wider.
A program may use at most 1 GiB of HBM per device.

v0:
```python
import jax
import jax.numpy as jnp
from jax import lax
from jax.sharding import PartitionSpec as P

EPS = 1e-6
HEAD = 128


def rms_norm(values, gain):
    scale = lax.rsqrt(jnp.mean(values * values, axis=-1, keepdims=True) + EPS)
    return (values * scale * gain).astype(jnp.bfloat16)


def attn_core(qkv_rows):
    num_seqs, seq_len, width = qkv_rows.shape
    heads = width // (3 * HEAD)
    split = qkv_rows.reshape(num_seqs, seq_len, 3, heads, HEAD)
    scores = jnp.einsum('bqhc,bkhc->bhqk', split[:, :, 0], split[:, :, 1], preferred_element_type=jnp.float32) * (HEAD ** -0.5)
    rows = lax.broadcasted_iota(jnp.int32, (seq_len, seq_len), 0)
    cols = lax.broadcasted_iota(jnp.int32, (seq_len, seq_len), 1)
    scores = jnp.where(rows >= cols, scores, -1e30)
    prob_rows = jax.nn.softmax(scores, axis=-1).astype(jnp.bfloat16)
    mixed = jnp.einsum('bhqk,bkhc->bqhc', prob_rows, split[:, :, 2], preferred_element_type=jnp.float32)
    return mixed.astype(jnp.bfloat16).reshape(num_seqs, seq_len, heads * HEAD)


def swiglu(gate_in, lin_in):
    return (jax.nn.silu(gate_in.astype(jnp.float32)) * lin_in.astype(jnp.float32)).astype(jnp.bfloat16)


def gate_weights(logits, idx_rows):
    prob_rows = jax.nn.softmax(logits, axis=-1)
    picked = jnp.take_along_axis(prob_rows, idx_rows, axis=-1)
    return picked / jnp.sum(picked, axis=-1, keepdims=True)


def route_tables(idx_rows, experts, cap):
    tokens, top = idx_rows.shape
    onehot = (idx_rows[:, :, None] == jnp.arange(experts, dtype=jnp.int32)[None, None, :]).astype(jnp.int32)
    counts = jnp.sum(onehot, axis=1)
    prior = jnp.cumsum(counts, axis=0) - counts
    position = jnp.sum(onehot * prior[:, None, :], axis=-1)
    slot = jnp.where(position < cap, idx_rows * cap + position, experts * cap)
    flat_ids = jnp.arange(tokens * top, dtype=jnp.int32)
    src_id = jnp.full((experts * cap + 1,), tokens * top, jnp.int32).at[slot.reshape(-1)].set(flat_ids)
    return slot, src_id[:experts * cap]


def solution(mesh):
    ep_size = mesh.shape['ep']
    tok_spec = P(('dp', 'ep'))
    exp_spec = P('ep')
    rep_spec = P()

    def local(x_in, dy_in, route_idx, gain_attn, w_qkv, w_o, gain_ffn, w_router, w_up, w_lin, w_down):
        num_seqs, seq_len, width = x_in.shape
        tokens = num_seqs * seq_len
        top = route_idx.shape[-1]
        experts = w_router.shape[1]
        local_exp = w_up.shape[0]
        cap = ((tokens * top * 5) // (experts * 4) + 7) // 8 * 8
        idx_rows = route_idx.reshape(tokens, top)
        x_f = x_in.astype(jnp.float32)
        xn_one, norm_one_pull = jax.vjp(rms_norm, x_f, gain_attn.astype(jnp.float32))
        qkv_all = jnp.einsum('bsd,de->bse', xn_one, w_qkv, preferred_element_type=jnp.float32).astype(jnp.bfloat16)
        attn_out, attn_pull = jax.vjp(attn_core, qkv_all)
        attn_proj = jnp.einsum('bsd,de->bse', attn_out, w_o, preferred_element_type=jnp.float32)
        hidden = (x_f + attn_proj).astype(jnp.bfloat16).astype(jnp.float32).reshape(tokens, width)
        xn_two, norm_two_pull = jax.vjp(rms_norm, hidden, gain_ffn.astype(jnp.float32))
        logits = jnp.dot(xn_two, w_router, preferred_element_type=jnp.float32)
        gates, gate_pull = jax.vjp(lambda logit_in: gate_weights(logit_in, idx_rows), logits)
        slot, src_id = route_tables(idx_rows, experts, cap)
        x_pad = jnp.concatenate([xn_two, jnp.zeros((1, width), jnp.bfloat16)], axis=0)
        send = x_pad[src_id // top].reshape(ep_size, local_exp, cap, width)
        recv = lax.all_to_all(send, 'ep', 0, 0)
        up_gate = jnp.einsum('secd,edf->secf', recv, w_up, preferred_element_type=jnp.float32).astype(jnp.bfloat16)
        up_lin = jnp.einsum('secd,edf->secf', recv, w_lin, preferred_element_type=jnp.float32).astype(jnp.bfloat16)
        act_rows, act_pull = jax.vjp(swiglu, up_gate, up_lin)
        y_exp = jnp.einsum('secf,efd->secd', act_rows, w_down, preferred_element_type=jnp.float32).astype(jnp.bfloat16)
        y_back = lax.all_to_all(y_exp, 'ep', 0, 0).reshape(experts * cap, width)
        y_pad = jnp.concatenate([y_back, jnp.zeros((1, width), jnp.bfloat16)], axis=0)
        y_sel = y_pad[slot]
        dy_rows = dy_in.reshape(tokens, width).astype(jnp.float32)
        d_gates = jnp.sum(dy_rows[:, None, :] * y_sel, axis=-1)
        d_ysel = (gates[:, :, None] * dy_rows[:, None, :]).astype(jnp.bfloat16).reshape(tokens * top, width)
        d_pad = jnp.concatenate([d_ysel, jnp.zeros((1, width), jnp.bfloat16)], axis=0)
        d_send = d_pad[src_id].reshape(ep_size, local_exp, cap, width)
        d_recv = lax.all_to_all(d_send, 'ep', 0, 0)
        d_act = jnp.einsum('secd,efd->secf', d_recv, w_down, preferred_element_type=jnp.float32).astype(jnp.bfloat16)
        grad_down = jnp.einsum('secf,secd->efd', act_rows, d_recv, preferred_element_type=jnp.float32)
        d_gate_in, d_lin_in = act_pull(d_act)
        grad_up = jnp.einsum('secd,secf->edf', recv, d_gate_in, preferred_element_type=jnp.float32)
        grad_lin = jnp.einsum('secd,secf->edf', recv, d_lin_in, preferred_element_type=jnp.float32)
        d_tok_exp = (jnp.einsum('secf,edf->secd', d_gate_in, w_up, preferred_element_type=jnp.float32) + jnp.einsum('secf,edf->secd', d_lin_in, w_lin, preferred_element_type=jnp.float32)).astype(jnp.bfloat16)
        d_back = lax.all_to_all(d_tok_exp, 'ep', 0, 0).reshape(experts * cap, width)
        d_back_pad = jnp.concatenate([d_back, jnp.zeros((1, width), jnp.bfloat16)], axis=0)
        d_moe_in = jnp.sum(d_back_pad[slot], axis=1, dtype=jnp.float32)
        d_logits = gate_pull(d_gates)[0]
        d_xn_two = (d_moe_in + jnp.einsum('te,de->td', d_logits, w_router, preferred_element_type=jnp.float32)).astype(jnp.bfloat16)
        grad_router = jnp.einsum('td,te->de', xn_two, d_logits, preferred_element_type=jnp.float32)
        d_hidden, grad_gain_ffn = norm_two_pull(d_xn_two)
        d_resid = (d_hidden + dy_rows).astype(jnp.bfloat16).reshape(num_seqs, seq_len, width)
        grad_wo = jnp.einsum('bsd,bse->de', attn_out, d_resid, preferred_element_type=jnp.float32)
        d_attn_out = jnp.einsum('bse,de->bsd', d_resid, w_o, preferred_element_type=jnp.float32).astype(jnp.bfloat16)
        d_qkv = attn_pull(d_attn_out)[0]
        grad_wqkv = jnp.einsum('bsd,bse->de', xn_one, d_qkv, preferred_element_type=jnp.float32)
        d_xn_one = jnp.einsum('bse,de->bsd', d_qkv, w_qkv, preferred_element_type=jnp.float32).astype(jnp.bfloat16)
        d_x_norm, grad_gain_attn = norm_one_pull(d_xn_one)
        dx_out = (d_x_norm + d_resid.astype(jnp.float32)).astype(jnp.bfloat16)
        dense = lax.psum((grad_gain_attn, grad_wqkv, grad_wo, grad_gain_ffn, grad_router), ('dp', 'ep'))
        expert_grads = lax.psum((grad_up, grad_lin, grad_down), 'dp')
        return (dx_out,) + tuple(dense) + tuple(expert_grads)

    in_specs = (tok_spec, tok_spec, tok_spec, rep_spec, rep_spec, rep_spec, rep_spec, rep_spec, exp_spec, exp_spec, exp_spec)
    out_specs = (tok_spec, rep_spec, rep_spec, rep_spec, rep_spec, rep_spec, exp_spec, exp_spec, exp_spec)
    return jax.shard_map(local, mesh=mesh, in_specs=in_specs, out_specs=out_specs, check_vma=False)
```

profile of v0, /device:TPU:0, one launch (start us, length us, event | category | flops | bytes accessed | tf_op | source)
XLA Modules:
  0.0 3522.3 jit_solution(8687569481789270030)
XLA Ops:
  19.4 10.6 convolution_convert_fusion
  41.0 10.0 gather_fusion.1
  58.3 12.7 gather_fusion.4
  78.2 11.7 mul.291
  96.8 16.2 gather_fusion
  113.0 15.4 all-to-all-done.1
  133.4 11.2 fusion.54
  144.6 11.1 fusion.44
  155.7 9.4 convert_bitcast_fusion
  168.2 36.7 %all-to-all-done = bf16[8,8,32,1536]{3,2,1,0:T(8,128)(2,1)} async-done(((bf16[8,8,32,1536]{3,2,1,0:T(8,128)(2,1)}), bf16[8,8,32,1536]{3,2,1,0:T(8,128)(2,1)}, u32[]{:S(2)}, u32[]{:S(2)}) %all-to-all-start) | async-done | bytes 6291488 | tf_op jit(solution)/shard_map/all_to_all | solution.py:89
  210.3 11.2 fusion.29
  221.5 13.5 fusion.1
  235.0 13.4 fusion.13
  254.7 27.1 all-to-all-done.3
  293.5 14.0 gather_fusion.3
  307.5 8.8 reshape.501
  323.0 8.6 scatter_custom_fusion.1
  332.7 25.3 all-to-all-done.2
  363.9 14.0 gather_fusion.2
  377.9 9.0 reshape.500
  416.6 12.2 fusion.83
  429.3 16.5 convolution_bitcast_fusion
  445.8 15.8 convolution_bitcast_fusion.1
  461.6 15.9 convolution_bitcast_fusion.2
  477.5 10.3 fusion.64
  487.9 41.4 %all-reduce.7 = (f32[1536]{0:T(1024)}, f32[1536]{0:T(1024)}) all-reduce(f32[1536]{0:T(1024)S(1)} %get-tuple-element.11, f32[1536]{0:T(1024)S(1)} %copy-done.35), channel_id=1, replica_groups=mesh['dp'=4,'ep'=8] {'dp','ep'}, use_global_device_ids=true, to_apply=%region_21.22 | all-reduce | flops 3072 | bytes 24576 | tf_op jit(solution)/shard_map/psum | solution.py:111
  532.3 451.8 %all-reduce.13.cloned.1.call-done = (f32[1536,4608]{1,0:T(8,128)}, f32[1536,1536]{1,0:T(8,128)}, f32[1536,64]{0,1:T(8,128)}) async-done(((f32[1536,4608]{1,0:T(8,128)}, f32[1536,1536]{1,0:T(8,128)}, f32[1536,64]{0,1:T(8,128)}), (f32[1536,4608]{1,0:T(8,128)}, f32[1536,1536]{1,0:T(8,128)}, f32[1536,64]{0,1:T(8,128)})) %all-reduce.13.cloned.1.call-update) | async-done | bytes 38141968 | tf_op jit(solution)/shard_map/psum | solution.py:111
  984.1 2456.7 %all-reduce.15.cloned.1.call-done = (f32[8,1536,512]{2,1,0:T(8,128)}, f32[8,1536,512]{2,1,0:T(8,128)}, f32[8,512,1536]{2,1,0:T(8,128)}) async-done(((f32[8,1536,512]{2,1,0:T(8,128)}, f32[8,1536,512]{2,1,0:T(8,128)}, f32[8,512,1536]{2,1,0:T(8,128)}), (f32[8,1536,512]{2,1,0:T(8,128)}, f32[8,1536,512]{2,1,0:T(8,128)}, f32[8,512,1536]{2,1,0:T(8,128)})) %all-reduce.15.cloned.1.call-update) | async-done | bytes 75497488 | tf_op jit(solution)/shard_map/psum | solution.py:112
  3440.8 21.0 copy.209
  3467.3 19.5 copy.212
  3486.8 19.5 copy.213
  3506.4 8.9 copy.214
  (215 shorter events, 127.6 us)
Async XLA Ops:
  7.2 50.6 %copy-start = (bf16[1536,64]{0,1:T(8,128)(2,1)S(1)}, bf16[1536,64]{0,1:T(8,128)(2,1)}, u32[]{:S(2)}) copy-start(bf16[1536,64]{0,1:T(8,128)(2,1)} %param.18) | copy-start | bytes 589828
  8.7 24.8 copy-start.31
  10.1 19.9 copy-start.37
  11.5 28.3 copy-start.25
  40.9 16.9 copy-start.8
  51.0 77.3 %all-to-all-start.1 = ((bf16[8,8,32,1536]{3,2,1,0:T(8,128)(2,1)}), bf16[8,8,32,1536]{3,2,1,0:T(8,128)(2,1)}, u32[]{:S(2)}, u32[]{:S(2)}) async-start(bf16[8,8,32,1536]{3,2,1,0:T(8,128)(2,1)} %bitcast.236), calls=%async_computation.1 | async-start | bytes 12582912 | tf_op jit(solution)/shard_map/all_to_all | solution.py:76
  58.2 12.8 copy-start.20
  58.2 12.8 copy-start.33
  58.3 13.3 copy-start.18
  128.3 76.6 %all-to-all-start = ((bf16[8,8,32,1536]{3,2,1,0:T(8,128)(2,1)}), bf16[8,8,32,1536]{3,2,1,0:T(8,128)(2,1)}, u32[]{:S(2)}, u32[]{:S(2)}) async-start(bf16[8,8,32,1536]{3,2,1,0:T(8,128)(2,1)} %bitcast.237), calls=%async_computation | async-start | bytes 12582912 | tf_op jit(solution)/shard_map/all_to_all | solution.py:89
  204.9 76.8 %all-to-all-start.3 = ((bf16[8,8,32,1536]{3,2,1,0:T(8,128)(2,1)}), bf16[8,8,32,1536]{3,2,1,0:T(8,128)(2,1)}, u32[]{:S(2)}, u32[]{:S(2)}) async-start(bf16[8,8,32,1536]{3,2,1,0:T(8,128)(2,1)} %copy.140), calls=%async_computation.3 | async-start | bytes 12582912 | tf_op jit(solution)/shard_map/all_to_all | solution.py:81
  254.6 32.1 copy-start.28
  254.6 32.1 copy-start.48
  254.6 32.2 copy-start.47
  254.6 32.6 copy-start.36
  254.6 32.9 copy-start.40
  254.7 32.9 copy-start.30
  281.8 76.2 %all-to-all-start.2 = ((bf16[8,8,32,1536]{3,2,1,0:T(8,128)(2,1)}), bf16[8,8,32,1536]{3,2,1,0:T(8,128)(2,1)}, u32[]{:S(2)}, u32[]{:S(2)}) async-start(bf16[8,8,32,1536]{3,2,1,0:T(8,128)(2,1)} %copy.134), calls=%async_computation.2 | async-start | bytes 12582912 | tf_op jit(solution)/shard_map/all_to_all | solution.py:96
  286.5 697.6 %all-reduce.13.cloned.1.call-start = ((), (), s32[]{:S(2)}) async-start(), calls=%async_computation.4 | async-start | bytes 76283904 | tf_op jit(solution)/shard_map/psum | solution.py:111
  316.3 15.3 copy-start.21
  316.3 15.3 copy-start.34
  316.3 15.4 copy-start.9
  397.4 12.8 copy-start.13
  428.8 3012.0 %all-reduce.15.cloned.1.call-start = ((), (), s32[]{:S(2)}) async-start(), calls=%async_computation.5 | async-start | bytes 150994944 | tf_op jit(solution)/shard_map/psum | solution.py:112
  477.5 51.8 %copy-start.44 = (f32[256]{0:T(256)S(1)}, f32[256]{0:T(256)}, u32[]{:S(2)}) copy-start(f32[256]{0:T(256)} %copy-done.43) | copy-start | bytes 3076
  3440.8 22.0 copy-start.10
  3467.3 39.0 %slice-start = ((s8[25165824]{0:T(1024)(128)(4,1)}), s8[4194304]{0:T(1024)(128)(4,1)S(1)}, s32[]{:S(2)}) async-start(s8[25165824]{0:T(1024)(128)(4,1)} %bitcast.234), calls=%async_computation.6 | async-start | bytes 8388608
  3467.3 39.0 %slice-start.1 = ((s8[25165824]{0:T(1024)(128)(4,1)}), s8[4194304]{0:T(1024)(128)(4,1)S(1)}, s32[]{:S(2)}) async-start(s8[25165824]{0:T(1024)(128)(4,1)} %bitcast.234), calls=%async_computation.7 | async-start | bytes 8388608
  3467.3 39.0 %slice-start.2 = ((s8[25165824]{0:T(1024)(128)(4,1)}), s8[4194304]{0:T(1024)(128)(4,1)S(1)}, s32[]{:S(2)}) async-start(s8[25165824]{0:T(1024)(128)(4,1)} %bitcast.234), calls=%async_computation.8 | async-start | bytes 8388608
  3486.8 19.5 slice-start.3
  3486.8 19.5 slice-start.4
  3486.8 19.5 slice-start.5
  (31 other events, 154.9 us)
Sparse Core Ops, SparseCore 0:
  428.9 555.1 all-reduce.12
  988.1 2452.6 all-reduce.14
where the time goes:
time: 3530 us; the launch traced here: 3520 us
  waiting for transfers between devices  3010 us (85%)
  local copies, waits for them, and re-layouts  221 us (6%)
  matrix products  172 us (5%)
  blocking collectives  41.4 us (1%)
  other arithmetic  38.8 us (1%)
    psum x1, waiting for transfers between devices, local(): expert_grads = lax.psum((grad_up, grad_lin, grad_down), 'dp')  2460 us
    psum x1, waiting for transfers between devices, local(): lax.psum((grad_gain_attn, grad_wqkv, grad_wo, grad_gain_ffn, grad_router)...  452 us
    unnamed x123, local copies, waits for them, and re-layouts  81 us
  transfers between devices with their start and end apart: 6, of which 6 were waited for; matrix products, arithmetic and copies ran while one was open for 7% of the time, Pallas kernels for 0%

commit v1 on v0

v1 whole, which is shorter than its diff:
```python
import jax
import jax.numpy as jnp
from jax import lax
from jax.sharding import PartitionSpec as P


EPS = 1e-6
HEAD = 128
DROPPED = 64.0
UNCHOSEN = 128.0
F32 = jnp.float32
BF16 = jnp.bfloat16


def mm(spec, a, b):
    return jnp.einsum(spec, a, b, preferred_element_type=F32)


def rms_norm(values, gain):
    scale = lax.rsqrt(jnp.mean(values * values, axis=-1, keepdims=True) + EPS)
    return (values * scale * gain).astype(BF16)


def attn_core(qkv_rows):
    num_seqs, seq_len, width = qkv_rows.shape
    heads = width // (3 * HEAD)
    split = qkv_rows.reshape(num_seqs, seq_len, 3, heads, HEAD)
    scores = mm('bqhc,bkhc->bhqk', split[:, :, 0], split[:, :, 1]) * (HEAD ** -0.5)
    rows = lax.broadcasted_iota(jnp.int32, (seq_len, seq_len), 0)
    cols = lax.broadcasted_iota(jnp.int32, (seq_len, seq_len), 1)
    scores = jnp.where(rows >= cols, scores, -1e30)
    prob_rows = jax.nn.softmax(scores, axis=-1).astype(BF16)
    mixed = mm('bhqk,bkhc->bqhc', prob_rows, split[:, :, 2])
    return mixed.astype(BF16).reshape(num_seqs, seq_len, heads * HEAD)


def swiglu(gate_in, lin_in):
    return (jax.nn.silu(gate_in.astype(F32)) * lin_in.astype(F32)).astype(BF16)


def slot_codes(idx_rows, experts, cap):
    tokens = idx_rows.shape[0]
    chosen = jnp.any(idx_rows[:, :, None] == jnp.arange(experts, dtype=jnp.int32), axis=1).astype(BF16)
    rows = lax.broadcasted_iota(jnp.int32, (tokens, tokens), 0)
    cols = lax.broadcasted_iota(jnp.int32, (tokens, tokens), 1)
    prior = mm('se,st->et', chosen, (rows < cols).astype(BF16))
    taken = mm('se,st->et', chosen, (rows == cols).astype(BF16))
    return jnp.where(taken > 0.5, jnp.where(prior < cap, prior, DROPPED), UNCHOSEN).astype(BF16)


def one_hot(codes, cap):
    slots = lax.broadcasted_iota(jnp.int32, codes.shape[:-1] + (cap, codes.shape[-1]), codes.ndim - 1)
    return (codes[..., None, :].astype(F32) == slots.astype(F32)).astype(BF16)


def gates_of(xn, codes, w_router):
    logits = mm('...td,de->...et', xn, w_router)
    prob = jax.nn.softmax(logits, axis=-2)
    mask = (codes.astype(F32) < UNCHOSEN - 1.0).astype(F32)
    picked = prob * mask
    total = jnp.sum(picked, axis=-2, keepdims=True)
    return prob, mask, picked / total, total


def dispatch(select, rows):
    return mm('sect,std->secd', select, rows).astype(BF16)


def expert_core(select, gate_rows, xn, dy, w_up, w_lin, w_down):
    recv = dispatch(select, xn)
    dy_rows = dispatch(select, dy)
    gate_slot = jnp.sum(select.astype(F32) * gate_rows[:, :, None, :], axis=-1, keepdims=True)
    d_recv = (gate_slot * dy_rows.astype(F32)).astype(BF16)
    up_gate = mm('secd,edf->secf', recv, w_up).astype(BF16)
    up_lin = mm('secd,edf->secf', recv, w_lin).astype(BF16)
    act_rows, act_pull = jax.vjp(swiglu, up_gate, up_lin)
    d_act = mm('secd,efd->secf', d_recv, w_down).astype(BF16)
    d_gate_in, d_lin_in = act_pull(d_act)
    return recv, dy_rows, d_recv, act_rows, d_gate_in, d_lin_in


def sum_everywhere(value, world):
    piece = lax.psum_scatter(value, world, scatter_dimension=0, tiled=True)
    return lax.all_gather(piece, world, axis=0, tiled=True)


def after(value, *deps):
    return lax.optimization_barrier((value,) + deps)[0]


def solution(mesh):
    tok_spec = P(('dp', 'ep'))
    exp_spec = P('ep')
    rep_spec = P()
    world = ('dp', 'ep')

    def local(x_in, dy_in, route_idx, gain_attn, w_qkv, w_o, gain_ffn, w_router, w_up, w_lin, w_down):
        num_seqs, seq_len, width = x_in.shape
        tokens = num_seqs * seq_len
        top = route_idx.shape[-1]
        experts = w_router.shape[1]
        local_exp = w_up.shape[0]
        cap = ((tokens * top * 5) // (experts * 4) + 7) // 8 * 8
        my_dp, my_ep = lax.axis_index('dp'), lax.axis_index('ep')
        ep_size = mesh.shape['ep']

        codes = slot_codes(route_idx.reshape(tokens, top), experts, cap)
        dy_own = dy_in.reshape(tokens, width)
        codes_all = lax.all_gather(codes, world)
        dy_plane = lax.all_gather(dy_own, 'ep')

        x_f = x_in.astype(F32)
        xn_one, norm_one_pull = jax.vjp(rms_norm, x_f, gain_attn.astype(F32))
        qkv_all = mm('bsd,de->bse', xn_one, w_qkv).astype(BF16)
        attn_out, attn_pull = jax.vjp(attn_core, qkv_all)
        attn_proj = mm('bsd,de->bse', attn_out, w_o)
        hidden = (x_f + attn_proj).astype(BF16).astype(F32).reshape(tokens, width)
        xn_two, norm_two_pull = jax.vjp(rms_norm, hidden, gain_ffn.astype(F32))

        xn_plane = lax.all_gather(after(xn_two, dy_plane, codes_all), 'ep')
        dy_all = lax.all_gather(after(dy_own, xn_plane), world)
        xn_all = lax.all_gather(after(xn_two, xn_plane), world)

        mine = lambda arr: lax.dynamic_slice_in_dim(arr, my_ep * local_exp, local_exp, axis=1)
        codes_plane = lax.dynamic_slice_in_dim(codes_all, my_dp * ep_size, ep_size, axis=0)
        _, _, gates_plane, _ = gates_of(xn_plane, codes_plane, w_router)
        recv, dy_rows, d_recv, act_rows, d_gate_in, d_lin_in = expert_core(
            one_hot(mine(codes_plane), cap), mine(gates_plane), xn_plane, dy_plane, w_up, w_lin, w_down)
        y_exp = mm('secf,efd->secd', act_rows, w_down).astype(BF16)
        d_gate_rows = jnp.sum(dy_rows.astype(F32) * y_exp.astype(F32), axis=-1)
        d_gate_back = lax.all_to_all(d_gate_rows, 'ep', 0, 0).reshape(experts, cap)
        d_tok_exp = (mm('secf,edf->secd', d_gate_in, w_up) + mm('secf,edf->secd', d_lin_in, w_lin)).astype(BF16)
        d_back = lax.all_to_all(d_tok_exp, 'ep', 0, 0).reshape(experts, cap, width)

        select_own = one_hot(codes, cap)
        d_moe_in = mm('ect,ecd->td', select_own, d_back)
        prob, mask, gates, total = gates_of(xn_two, codes, w_router)
        d_gates = jnp.sum(select_own.astype(F32) * d_gate_back[:, :, None], axis=1)
        d_picked = (d_gates - jnp.sum(d_gates * gates, axis=0, keepdims=True)) / total * mask
        d_logits = (prob * (d_picked - jnp.sum(prob * d_picked, axis=0, keepdims=True))).astype(BF16)
        d_xn_two = (d_moe_in + mm('et,de->td', d_logits, w_router)).astype(BF16)
        grad_router = mm('td,et->de', xn_two, d_logits)
        grad_router = lax.psum(grad_router, world)
        d_hidden, grad_gain_ffn = norm_two_pull(d_xn_two)
        d_resid = (d_hidden + dy_own.astype(F32)).astype(BF16).reshape(num_seqs, seq_len, width)
        grad_wo = mm('bsd,bse->de', attn_out, d_resid)
        d_attn_out = mm('bse,de->bsd', d_resid, w_o).astype(BF16)
        grad_wo = sum_everywhere(grad_wo, world)
        d_qkv = attn_pull(d_attn_out)[0]
        grad_wqkv = mm('bsd,bse->de', xn_one, d_qkv)
        piece_wqkv = lax.psum_scatter(grad_wqkv, world, scatter_dimension=0, tiled=True)
        grad_wqkv = lax.all_gather(piece_wqkv, world, axis=0, tiled=True)
        d_xn_one = mm('bse,de->bsd', d_qkv, w_qkv).astype(BF16)
        d_x_norm, grad_gain_attn = norm_one_pull(d_xn_one)
        dx_out = (d_x_norm + d_resid.astype(F32)).astype(BF16)
        grad_gain_attn, grad_gain_ffn = lax.psum((grad_gain_attn, grad_gain_ffn), world)

        xn_late = after(xn_all, d_qkv)
        _, _, gates_all, _ = gates_of(xn_late, codes_all, w_router)
        recv, dy_rows, d_recv, act_rows, d_gate_in, d_lin_in = expert_core(
            one_hot(mine(codes_all), cap), mine(gates_all), xn_late, dy_all, w_up, w_lin, w_down)
        grad_down = mm('secf,secd->efd', act_rows, d_recv)
        grad_up = mm('secd,secf->edf', recv, d_gate_in)
        grad_lin = mm('secd,secf->edf', recv, d_lin_in)
        return (dx_out, grad_gain_attn, grad_wqkv, grad_wo, grad_gain_ffn, grad_router, grad_up, grad_lin, grad_down)

    in_specs = (tok_spec, tok_spec, tok_spec, rep_spec, rep_spec, rep_spec, rep_spec, rep_spec, exp_spec, exp_spec, exp_spec)
    out_specs = (tok_spec, rep_spec, rep_spec, rep_spec, rep_spec, rep_spec, exp_spec, exp_spec, exp_spec)

    return jax.shard_map(local, mesh=mesh, in_specs=in_specs, out_specs=out_specs, check_vma=False)
```

time: 3530 us -> 1490 us (0.42)
  waiting for transfers between devices: 3010 us -> 983 us
  matrix products: 172 us -> 379 us
  local copies, waits for them, and re-layouts: 221 us -> 40.8 us
    psum x2 -> x1, waiting for transfers between devices: 2910 us -> 133 us  [local(): grad_router = lax.psum(grad_router, world)]
    all_gather x0 -> x7, waiting for transfers between devices: none -> 402 us  [the longest x1 156 us: local(): xn_all = lax.all_gather(after(xn_two, xn_plane), world)]
    reduce_scatter x0 -> x2, waiting for transfers between devices: none -> 378 us  [the longest x1 267 us: local(): lax.psum_scatter(grad_wqkv, world, scatter_dimension=0, tiled=True)]
    dot_general x24 -> x35, matrix products: 172 us -> 374 us  [mm(): return jnp.einsum(spec, a, b, preferred_element_type=F32)]
    gather x9 -> x0, local copies, waits for them, and re-layouts: 67.3 us -> none  [the longest x1 16.2 us: local(): d_send = d_pad[src_id].reshape(ep_size, local_exp, cap, width)]
    unnamed x123 -> x82, local copies, waits for them, and re-layouts: 81 us -> 30.6 us
    all_to_all x4 -> x2, waiting for transfers between devices: 104 us -> 68.2 us  [the longest x1 68.2 us: local(): d_back = lax.all_to_all(d_tok_exp, 'ep', 0, 0).reshape(experts, cap, width)]
  transfers between devices with their start and end apart: 6 -> 12, of which waited for: 6 -> 11; matrix products, arithmetic and copies ran while one was open for 7% -> 22% of each run, Pallas kernels for 0% -> 0%
where the time goes in v1:
time: 1490 us
  waiting for transfers between devices  983 us (66%)
  matrix products  379 us (25%)
  blocking collectives  42.1 us (3%)
  local copies, waits for them, and re-layouts  40.8 us (3%)
  other arithmetic  18.3 us (1%)
  between operations  15 us (1%)
    dot_general x35, matrix products, mm(): return jnp.einsum(spec, a, b, preferred_element_type=F32)  374 us
    reduce_scatter x1, waiting for transfers between devices, local(): lax.psum_scatter(grad_wqkv, world, scatter_dimension=0, tiled=True)  267 us
    all_gather x1, waiting for transfers between devices, local(): xn_all = lax.all_gather(after(xn_two, xn_plane), world)  156 us
    psum x1, waiting for transfers between devices, local(): grad_router = lax.psum(grad_router, world)  133 us
    reduce_scatter x1, waiting for transfers between devices, sum_everywhere(): piece = lax.psum_scatter(value, world, scatter_dimension=0, tiled=True)  111 us
    all_gather x1, waiting for transfers between devices, local(): dy_all = lax.all_gather(after(dy_own, xn_plane), world)  68.7 us
    all_to_all x1, waiting for transfers between devices, local(): d_back = lax.all_to_all(d_tok_exp, 'ep', 0, 0).reshape(experts, cap, width)  68.2 us
    all_gather x1, waiting for transfers between devices, local(): xn_plane = lax.all_gather(after(xn_two, dy_plane, codes_all), 'ep')  46.4 us
  transfers between devices with their start and end apart: 12, of which 11 were waited for; matrix products, arithmetic and copies ran while one was open for 22% of the time, Pallas kernels for 0%

profile of v1, /device:TPU:0, one launch (start us, length us, event | category | flops | bytes accessed | tf_op | source)
XLA Modules:
  0.0 1487.3 jit_solution(15209178492723199975)
XLA Ops:
  13.7 10.6 convolution_convert_fusion
  35.1 32.2 %all-gather.18.cloned.1.call-done = bf16[2048,256]{1,0:T(8,128)(2,1)} async-done(((bf16[64,256]{1,0:T(8,128)(2,1)}), bf16[2048,256]{1,0:T(8,128)(2,1)}) %all-gather.18.cloned.1.call-update) | async-done | bytes 1048592 | tf_op jit(solution)/shard_map/all_gather | solution.py:109
  67.2 46.3 %all-gather.12.cloned.1.call-done = bf16[8,256,1536]{2,1,0:T(8,128)(2,1)} async-done(((bf16[1,256,1536]{2,1,0:T(8,128)(2,1)}), bf16[8,256,1536]{2,1,0:T(8,128)(2,1)}) %all-gather.12.cloned.1.call-update) | async-done | bytes 6291472 | tf_op jit(solution)/shard_map/all_gather | solution.py:110
  114.5 46.4 %all-gather.20.cloned.1.call-done = bf16[2048,1536]{1,0:T(8,128)(2,1)} async-done(((bf16[256,1536]{1,0:T(8,128)(2,1)}), bf16[2048,1536]{1,0:T(8,128)(2,1)}) %all-gather.20.cloned.1.call-update) | async-done | bytes 6291472 | tf_op jit(solution)/shard_map/all_gather | solution.py:120
  170.8 9.2 fusion.127
  180.0 10.5 fusion.85
  197.2 8.9 fusion.30
  206.8 11.2 fusion.122
  221.4 16.7 %fusion.32 = f32[8,8,32,1536]{3,2,1,0:T(8,128)} fusion(bf16[8,1536,512]{2,1,0:T(8,128)(2,1)} %param.19, bf16[8,8,32,512]{3,2,1,0:T(8,128)(2,1)} %fusion.127, bf16[8,8,32,512]{3,2,1,0:T(8,128)(2,1)} %get-tuple-element.38, bf16[8,8,32,512]{3,2,1,0:T(8,128)(2,1)} %fusion.122), kind=kOutput, calls=%fused_computation.41 | convolution fusion | flops 3235905536 | bytes 31457280 | tf_op jit(solution)/shard_map/secf,edf->secd/dot_general | solution.py:16
  238.1 14.2 fusion.64
  266.7 68.2 %all-to-all-done = bf16[8,8,32,1536]{3,2,1,0:T(8,128)(2,1)} async-done(((bf16[8,8,32,1536]{3,2,1,0:T(8,128)(2,1)}), bf16[8,8,32,1536]{3,2,1,0:T(8,128)(2,1)}, u32[]{:S(2)}, u32[]{:S(2)}) %all-to-all-start) | async-done | bytes 6291488 | tf_op jit(solution)/shard_map/all_to_all | solution.py:133
  334.9 10.1 fusion.99
  363.8 12.6 fusion.170
  376.4 111.2 %reduce-scatter.5.cloned.1.call-done = f32[48,1536]{1,0:T(8,128)} async-done(((f32[1536,1536]{1,0:T(8,128)}), f32[48,1536]{1,0:T(8,128)}) %reduce-scatter.5.cloned.1.call-update) | async-done | bytes 294928 | tf_op jit(solution)/shard_map/reduce_scatter | solution.py:83
  489.2 266.9 %reduce-scatter.3.cloned.1.call-done = f32[48,4608]{1,0:T(8,128)} async-done(((f32[1536,4608]{1,0:T(8,128)}), f32[48,4608]{1,0:T(8,128)}) %reduce-scatter.3.cloned.1.call-update) | async-done | bytes 884752 | tf_op jit(solution)/shard_map/reduce_scatter | solution.py:151
  758.9 9.4 fusion.137
  769.7 42.1 %all-reduce.3 = (f32[1536]{0:T(1024)}, f32[1536]{0:T(1024)}) all-reduce(f32[1536]{0:T(1024)S(1)} %get-tuple-element.17, f32[1536]{0:T(1024)S(1)} %copy-done.22), channel_id=1, replica_groups=mesh['dp'=4,'ep'=8] {'dp','ep'}, use_global_device_ids=true, to_apply=%region_20.21 | all-reduce | flops 3072 | bytes 24576 | tf_op jit(solution)/shard_map/psum | solution.py:156
  811.9 28.3 %all-gather.16.cloned.1.call-done = f32[1536,1536]{1,0:T(8,128)} async-done(((f32[48,1536]{1,0:T(8,128)}), f32[1536,1536]{1,0:T(8,128)}) %all-gather.16.cloned.1.call-update) | async-done | bytes 9437200 | tf_op jit(solution)/shard_map/all_gather | solution.py:84
  840.2 155.6 %all-gather.22.cloned.1.call-done = bf16[8192,1536]{1,0:T(8,128)(2,1)} async-done(((bf16[256,1536]{1,0:T(8,128)(2,1)}), bf16[8192,1536]{1,0:T(8,128)(2,1)}) %all-gather.22.cloned.1.call-update) | async-done | bytes 25165840 | tf_op jit(solution)/shard_map/all_gather | solution.py:122
  995.8 12.4 fusion.173
  1008.2 22.1 %fusion.13 = bf16[32,8,32,1536]{3,2,1,0:T(8,128)(2,1)} fusion(bf16[32,256,1536]{2,1,0:T(8,128)(2,1)} %bitcast.315, f32[32,8,256]{2,1,0:T(8,128)S(1)} %copy-done.15, f32[32]{0:T(128)S(1)} %iota_convert_fusion), kind=kOutput, calls=%fused_computation.15 | convolution fusion | flops 6457131008 | bytes 50593920 | tf_op jit(solution)/shard_map/sect,std->secd/dot_general | solution.py:16
  1030.2 23.1 %fusion.59 = bf16[8,32,32,512]{3,2,1,0:T(8,128)(2,1)} fusion(bf16[8,1536,512]{2,1,0:T(8,128)(2,1)} %param.19, bf16[32,8,32,1536]{3,2,1,0:T(8,128)(2,1)} %fusion.13), kind=kOutput, calls=%fused_computation.61 | convolution fusion | flops 12889096192 | bytes 46137344 | tf_op jit(solution)/shard_map/secd,edf->secf/dot_general | solution.py:16
  1053.4 22.9 %fusion.54 = bf16[8,32,32,512]{3,2,1,0:T(8,128)(2,1)} fusion(bf16[8,1536,512]{2,1,0:T(8,128)(2,1)} %param.20, bf16[32,8,32,1536]{3,2,1,0:T(8,128)(2,1)} %fusion.13), kind=kOutput, calls=%fused_computation.60 | convolution fusion | flops 12889096192 | bytes 46137344 | tf_op jit(solution)/shard_map/secd,edf->secf/dot_general | solution.py:16
  1082.1 68.7 %all-gather.24.cloned.1.call-done = bf16[8192,1536]{1,0:T(8,128)(2,1)} async-done(((bf16[256,1536]{1,0:T(8,128)(2,1)}), bf16[8192,1536]{1,0:T(8,128)(2,1)}) %all-gather.24.cloned.1.call-update) | async-done | bytes 25165840 | tf_op jit(solution)/shard_map/all_gather | solution.py:121
  1150.9 29.4 %multiply_convert_fusion = bf16[32,8,32,1536]{3,2,1,0:T(8,128)(2,1)} fusion(f32[32,8,32]{2,1,0:T(8,128)S(1)} %multiply_reduce_fusion, bf16[32,256,1536,1]{2,1,3,0:T(8,128)(2,1)} %bitcast.316, f32[32,8,256]{2,1,0:T(8,128)S(1)} %copy-done.15, f32[32]{0:T(128)S(1)} %iota_convert_fusion), kind=kOutput, calls=%fused_computation.3 | convolution fusion | flops 6494879744 | bytes 50626688 | tf_op jit(solution)/shard_map/sect,std->secd/dot_general | solution.py:16
  1180.3 29.5 %fusion.26 = (bf16[32,8,32,512]{3,2,0,1:T(8,128)(2,1)}, bf16[32,8,32,512]{3,2,0,1:T(8,128)(2,1)}) fusion(bf16[8,32,32,512]{3,2,1,0:T(8,128)(2,1)} %fusion.59, bf16[8,32,32,512]{3,2,1,0:T(8,128)(2,1)} %fusion.54, bf16[8,512,1536]{2,1,0:T(8,128)(2,1)} %param.21, bf16[32,8,32,1536]{3,2,1,0:T(8,128)(2,1)} %multiply_convert_fusion), kind=kOutput, calls=%fused_computation.32 | convolution fusion | flops 12960399360 | bytes 71303168 | tf_op jit(solution)/shard_map/secd,efd->secf/dot_general | solution.py:16
  1209.8 25.0 %convolution_bitcast_fusion = f32[8,1536,512]{2,1,0:T(8,128)} fusion(bf16[32,8,32,1536]{3,2,1,0:T(8,128)(2,1)} %fusion.13, bf16[32,8,32,512]{3,2,0,1:T(8,128)(2,1)} %get-tuple-element.23), kind=kOutput, calls=%fused_computation.16 | convolution fusion | flops 12884901888 | bytes 58720256 | tf_op jit(solution)/shard_map/secd,secf->edf/dot_general | solution.py:16
  1234.8 29.0 %convolution_bitcast_fusion.1 = f32[8,1536,512]{2,1,0:T(8,128)} fusion(bf16[32,8,32,1536]{3,2,1,0:T(8,128)(2,1)} %fusion.13, bf16[32,8,32,512]{3,2,0,1:T(8,128)(2,1)} %get-tuple-element.24), kind=kOutput, calls=%fused_computation.17 | convolution fusion | flops 12884901888 | bytes 58720256 | tf_op jit(solution)/shard_map/secd,secf->edf/dot_general | solution.py:16
  1263.7 32.6 %fusion.16 = f32[8,512,1536]{2,1,0:T(8,128)} fusion(bf16[32,8,32,1536]{3,2,1,0:T(8,128)(2,1)} %multiply_convert_fusion, bf16[8,32,32,512]{3,2,1,0:T(8,128)(2,1)} %fusion.54, bf16[8,32,32,512]{3,2,1,0:T(8,128)(2,1)} %fusion.59), kind=kOutput, calls=%fused_computation.18 | convolution fusion | flops 12918456320 | bytes 67108864 | tf_op jit(solution)/shard_map/secf,secd->efd/dot_general | solution.py:16
  1296.3 24.8 %all-gather.14.cloned.1.call-done = f32[1536,4608]{1,0:T(8,128)} async-done(((f32[48,4608]{1,0:T(8,128)}), f32[1536,4608]{1,0:T(8,128)}) %all-gather.14.cloned.1.call-update) | async-done | bytes 28311568 | tf_op jit(solution)/shard_map/all_gather | solution.py:152
  1321.1 132.6 %all-reduce.6.cloned.1.call-done = f32[1536,64]{0,1:T(8,128)} async-done(((f32[1536,64]{0,1:T(8,128)}), f32[1536,64]{0,1:T(8,128)}) %all-reduce.6.cloned.1.call-update) | async-done | bytes 393232 | tf_op jit(solution)/shard_map/psum | solution.py:143
  1453.7 21.0 %copy.194 = f32[1536,4608]{1,0:T(8,128)} copy(f32[1536,4608]{1,0:T(8,128)} %all-gather.14.cloned.1.call-done) | data formatting | bytes 56623104
  (158 shorter events, 88.8 us)
Async XLA Ops:
  7.2 153.7 %copy-start = (bf16[1536,64]{0,1:T(8,128)(2,1)S(1)}, bf16[1536,64]{0,1:T(8,128)(2,1)}, u32[]{:S(2)}) copy-start(bf16[1536,64]{0,1:T(8,128)(2,1)} %param.18) | copy-start | bytes 589828
  7.2 60.0 %all-gather.18.cloned.1.call-start = ((), (), s32[]{:S(2)}) async-start(), calls=%async_computation.10 | async-start | bytes 1081344 | tf_op jit(solution)/shard_map/all_gather | solution.py:109
  9.0 104.5 %all-gather.12.cloned.1.call-start = ((), (), s32[]{:S(2)}) async-start(), calls=%async_computation.4 | async-start | bytes 7077888 | tf_op jit(solution)/shard_map/all_gather | solution.py:110
  9.8 151.1 %all-gather.20.cloned.1.call-start = ((), (), s32[]{:S(2)}) async-start(), calls=%async_computation.11 | async-start | bytes 7077888 | tf_op jit(solution)/shard_map/all_gather | solution.py:120
  27.4 4.9 slice-start
  33.9 126.9 %copy-start.33 = (f32[256]{0:T(256)}, f32[256]{0:T(256)S(1)}, u32[]{:S(2)}) copy-start(f32[256]{0:T(256)S(1)} %get-tuple-element.27) | copy-start | bytes 3076
  33.9 79.6 %copy-start.27 = (f32[256]{0:T(256)}, f32[256]{0:T(256)S(1)}, u32[]{:S(2)}) copy-start(f32[256]{0:T(256)S(1)} %fusion.186) | copy-start | bytes 3076
  190.5 6.8 copy-start.35
  218.0 40.4 %all-to-all-start.1 = ((f32[8,1,256]{2,1,0:T(1,128)}), f32[8,1,256]{2,1,0:T(1,128)S(1)}, u32[]{:S(2)}, u32[]{:S(2)}) async-start(f32[8,1,256]{2,1,0:T(1,128)} %reshape.270), calls=%async_computation.1 | async-start | bytes 16384 | tf_op jit(solution)/shard_map/all_to_all | solution.py:131
  258.5 5.1 copy-start.2
  258.5 5.5 copy-start.19
  258.5 76.5 %all-to-all-start = ((bf16[8,8,32,1536]{3,2,1,0:T(8,128)(2,1)}), bf16[8,8,32,1536]{3,2,1,0:T(8,128)(2,1)}, u32[]{:S(2)}, u32[]{:S(2)}) async-start(bf16[8,8,32,1536]{3,2,1,0:T(8,128)(2,1)} %copy.105), calls=%async_computation | async-start | bytes 12582912 | tf_op jit(solution)/shard_map/all_to_all | solution.py:133
  263.4 224.2 %reduce-scatter.5.cloned.1.call-start = ((), (), s32[]{:S(2)}) async-start(), calls=%async_computation.7 | async-start | bytes 9732096 | tf_op jit(solution)/shard_map/reduce_scatter | solution.py:83
  266.7 78.4 %copy-start.25 = (f32[256]{0:T(256)}, f32[256]{0:T(256)S(1)}, u32[]{:S(2)}) copy-start(f32[256]{0:T(256)S(1)} %multiply_reduce_fusion.3) | copy-start | bytes 3076
  266.7 78.3 %copy-start.29 = (f32[256]{0:T(256)}, f32[256]{0:T(256)S(1)}, u32[]{:S(2)}) copy-start(f32[256]{0:T(256)S(1)} %fusion.176) | copy-start | bytes 3076
  334.9 10.1 copy-start.28
  347.0 5.5 copy-start.12
  352.1 404.0 %reduce-scatter.3.cloned.1.call-start = ((), (), s32[]{:S(2)}) async-start(), calls=%async_computation.5 | async-start | bytes 29196288 | tf_op jit(solution)/shard_map/reduce_scatter | solution.py:151
  376.4 381.4 %copy-start.3 = (bf16[256,1536]{1,0:T(8,128)(2,1)S(1)}, bf16[256,1536]{1,0:T(8,128)(2,1)}, u32[]{:S(2)}) copy-start(bf16[256,1536]{1,0:T(8,128)(2,1)} %fusion.138) | copy-start | bytes 2359300
  376.4 381.5 %copy-start.26 = (f32[256]{0:T(256)S(1)}, f32[256]{0:T(256)}, u32[]{:S(2)}) copy-start(f32[256]{0:T(256)} %copy-done.25) | copy-start | bytes 3076
  376.4 381.5 %copy-start.30 = (f32[256]{0:T(256)S(1)}, f32[256]{0:T(256)}, u32[]{:S(2)}) copy-start(f32[256]{0:T(256)} %copy-done.29) | copy-start | bytes 3076
  376.4 463.8 %all-gather.16.cloned.1.call-start = ((), (), s32[]{:S(2)}) async-start(), calls=%async_computation.8 | async-start | bytes 9732096 | tf_op jit(solution)/shard_map/all_gather | solution.py:84
  487.6 508.1 %all-gather.22.cloned.1.call-start = ((), (), s32[]{:S(2)}) async-start(), calls=%async_computation.12 | async-start | bytes 25952256 | tf_op jit(solution)/shard_map/all_gather | solution.py:122
  488.4 662.5 %all-gather.24.cloned.1.call-start = ((), (), s32[]{:S(2)}) async-start(), calls=%async_computation.13 | async-start | bytes 25952256 | tf_op jit(solution)/shard_map/all_gather | solution.py:121
  489.1 832.0 %all-gather.14.cloned.1.call-start = ((), (), s32[]{:S(2)}) async-start(), calls=%async_computation.6 | async-start | bytes 29196288 | tf_op jit(solution)/shard_map/all_gather | solution.py:152
  756.1 697.5 %all-reduce.6.cloned.1.call-start = ((), (), s32[]{:S(2)}) async-start(), calls=%async_computation.9 | async-start | bytes 786432 | tf_op jit(solution)/shard_map/psum | solution.py:143
  758.8 9.5 copy-start.32
  758.9 9.5 copy-start.11
  758.9 9.5 copy-start.13
  758.9 10.9 copy-start.22
  995.8 12.4 copy-start.15
  1453.7 22.0 %copy-start.8 = (f32[1536,1536]{1,0:T(8,128)S(1)}, f32[1536,1536]{1,0:T(8,128)}, u32[]{:S(2)}) copy-start(f32[1536,1536]{1,0:T(8,128)} %all-gather.16.cloned.1.call-done) | copy-start | bytes 28311556
  (18 other events, 45.7 us)
Sparse Core Ops, SparseCore 0:
  10.9 56.3 all-gather.17
  69.1 44.3 all-gather.11
  115.4 45.3 all-gather.19
  352.3 135.2 reduce-scatter.4
  494.4 261.6 reduce-scatter.2
  758.9 81.2 all-gather.15
  843.0 152.6 all-gather.21
  998.6 152.1 all-gather.23
  1153.8 167.2 all-gather.13
  1326.8 126.8 all-reduce.5
